TPU v7x, 32 devices: a whole 2x2x4 slice. The times are simulated.
32 devices in a mesh: grp: 4 (over z), dev: 8 (over y, x, core).
Axes of the slice: x: 2, y: 2, z: 4, core: 2. Of those that a mesh axis runs over, the one named last changes fastest.
Arguments:
- atm_state: float32 [4, 8, 128, 1024], P('grp', 'dev'), may hold values from -6 to 6
- atm_nbrs: int32 [4, 8, 4, 1024], P('grp', 'dev'), may hold values from 0 to 1279
- atm_send: int32 [4, 8, 256], P('grp', 'dev'), may hold values from 0 to 1023
- atm_mix: float32 [4, 8, 1024], P('grp', 'dev'), may hold values from 0.2 to 0.6
- flux_weight: float32 [24, 128], replicated, may hold values from -0.5 to 0.5
- margin_counts: int32 [4, 8, 1024], P('grp', 'dev'), may hold values from 1 to 4, 1536 in all within a row
- margin_weight: float32 [4, 8, 1536], P('grp', 'dev'), may hold values from 0.05 to 1
- block_owner: int32 [4, 8, 12, 1], P('grp', 'dev'), may hold values from 0 to 1, as said below
- recv_cols: int32 [4, 8, 2, 12, 128], P('grp', 'dev'), may hold values from 0 to 2047
- ocn_state: float32 [4, 8, 80, 2048], P('grp', 'dev'), may hold values from -6 to 6
- ocn_nbrs: int32 [4, 8, 6, 2048], P('grp', 'dev'), may hold values from 0 to 2303
- ocn_send: int32 [4, 8, 256], P('grp', 'dev'), may hold values from 0 to 2047
- ocn_mix: float32 [4, 8, 2048], P('grp', 'dev'), may hold values from 0.1 to 0.4
- force_weight: float32 [80, 24], replicated, may hold values from -1.25 to 1.25
- ret_weight: float32 [12, 80], replicated, may hold values from -0.625 to 0.625
Outputs:
- atm_next: float32 [4, 8, 128, 1024], P('grp', 'dev')
- ocn_next: float32 [4, 8, 80, 2048], P('grp', 'dev')
- atm_remapped: float32 [4, 8, 12, 1024], P('grp', 'dev')
Inputs may be any that keep to these rules, and one draw needn't show every extreme that they name: `margin_counts`: the 1024 counts of one partition sum to 1536, and one of them equals 4. `block_owner`: no partition sends more than 12 of its 12 blocks to one ocean group, and every partition sends exactly 12 blocks to one of them.
All inputs are finite; a program needn't handle non-finite values.
Results may differ from a plain program's by a relative error of at most 0.0029.
Values may be sent and summed in bfloat16 or wider, within the bound.
A program may use at most 64 MiB of HBM per device.

v0:
```python
import jax
import jax.numpy as jnp
from jax import lax
from jax.sharding import PartitionSpec as P

EXACT_DOT = lax.Precision.HIGHEST


def extended_2(shard, sides, width):
    for axis, dim in sides:
        peers, length = (lax.axis_size(axis), shard.shape[dim])
        up = [(i, (i + 1) % peers) for i in range(peers)]
        down = [(j, i) for i, j in up]
        last = lax.slice_in_dim(shard, length - width, length, axis=dim)
        leading = lax.slice_in_dim(shard, 0, width, axis=dim)
        before = lax.ppermute(last, axis, up)
        after = lax.ppermute(leading, axis, down)
        shard = jnp.concatenate([before, shard, after], axis=dim)
    return shard


def stencil(state, pool, neighbours, mixing):
    total = jnp.take(pool, neighbours[0], axis=1)
    for which in range(1, neighbours.shape[0]):
        total = total + jnp.take(pool, neighbours[which], axis=1)
    return state + mixing[None, :] * (total / neighbours.shape[0] - state)


def block_slots(owner):
    order = jnp.arange(owner.shape[0], dtype=jnp.int32)
    earlier = (owner[None, :] == owner[:, None]) & (order[None, :] < order[:, None])
    return jnp.sum(earlier.astype(jnp.int32), axis=1)


def with_rims(state, extended, half):
    return jnp.concatenate([state, extended[:, :half], extended[:, 3 * half :]], axis=1)


def on_device(
    atm_state,
    atm_nbrs,
    atm_send,
    atm_mix,
    flux_weight,
    margin_counts,
    margin_weight,
    block_owner,
    recv_cols,
    ocn_state,
    ocn_nbrs,
    ocn_send,
    ocn_mix,
    force_weight,
    ret_weight,
):
    atmosphere = atm_state[0, 0]
    ocean = ocn_state[0, 0]
    half = atm_send.shape[2] // 2
    levels_air = atmosphere.shape[0]
    groups = lax.axis_size("grp")
    atm_groups = recv_cols.shape[2]
    group = lax.axis_index("grp")
    air_here = group < atm_groups
    air_packed = jnp.take(atmosphere, atm_send[0, 0], axis=1)
    sea_packed = jnp.take(ocean, ocn_send[0, 0], axis=1)
    both_ext = extended_2(
        jnp.concatenate([air_packed, sea_packed], axis=0).astype(jnp.bfloat16), (("dev", 1),), half
    ).astype(jnp.float32)
    air_ext = both_ext[:levels_air]
    sea_ext = both_ext[levels_air:]
    atm_next = lax.cond(
        air_here,
        lambda: stencil(
            atmosphere, with_rims(atmosphere, air_ext, half), atm_nbrs[0, 0], atm_mix[0, 0]
        ),
        lambda: atmosphere,
    )
    ocn_base = lax.cond(
        air_here,
        lambda: ocean,
        lambda: stencil(ocean, with_rims(ocean, sea_ext, half), ocn_nbrs[0, 0], ocn_mix[0, 0]),
    )
    capacity = recv_cols.shape[3]
    block = recv_cols.shape[4]
    columns = atmosphere.shape[1]
    row_count = margin_weight.shape[2]
    blocks_here = block_owner.shape[2]
    fields = flux_weight.shape[0]
    ret_fields = ret_weight.shape[0]
    cells = ocean.shape[1]
    column = jnp.repeat(
        jnp.arange(columns, dtype=jnp.int32), margin_counts[0, 0], total_repeat_length=row_count
    )
    weights = margin_weight[0, 0]
    fluxes = jnp.dot(flux_weight, atm_next, precision=EXACT_DOT)
    row_values = (jnp.take(fluxes, column, axis=1) * weights[None, :]).astype(jnp.bfloat16)
    outgoing = row_values.reshape(fields, blocks_here, block).transpose(1, 0, 2)
    owner = block_owner[0, 0, :, 0]
    slot = block_slots(owner)
    cell_index = recv_cols[0, 0].reshape(-1)
    returned = jnp.dot(ret_weight, ocean, precision=EXACT_DOT).astype(jnp.bfloat16)
    looked = (
        jnp.take(returned, cell_index, axis=1)
        .reshape(ret_fields, atm_groups, capacity, block)
        .transpose(1, 2, 0, 3)
    )
    upward = (
        jnp.zeros((groups, capacity, fields, block), jnp.bfloat16)
        .at[atm_groups + owner, slot]
        .set(outgoing)
    )
    downward = jnp.concatenate(
        [looked, jnp.zeros((groups - atm_groups, capacity, ret_fields, block), jnp.bfloat16)],
        axis=0,
    )
    from_air = lax.all_to_all(upward, "grp", split_axis=0, concat_axis=0, tiled=True)[:atm_groups]
    from_owners = lax.all_to_all(downward, "grp", split_axis=0, concat_axis=0, tiled=True)[
        atm_groups:
    ]
    sea_side = (group >= atm_groups).astype(jnp.float32)
    air_side = 1.0 - sea_side
    incoming = from_air.transpose(2, 0, 1, 3).reshape(fields, -1).astype(jnp.float32)
    cell_flux = jnp.zeros((fields, cells), jnp.float32).at[:, cell_index].add(incoming)
    forcing = jnp.dot(force_weight, cell_flux, precision=EXACT_DOT)
    ocn_next = ocn_base + sea_side * forcing
    mine = (
        from_owners[owner, slot]
        .transpose(1, 0, 2)
        .reshape(ret_fields, row_count)
        .astype(jnp.float32)
    )
    weighted = (
        jnp.zeros((ret_fields, columns), jnp.float32).at[:, column].add(mine * weights[None, :])
    )
    weight_sum = jnp.zeros((columns,), jnp.float32).at[column].add(weights)
    remapped = air_side * (weighted / weight_sum[None, :])
    return (atm_next[None, None], ocn_next[None, None], remapped[None, None])


def solution(mesh):
    in_specs = (
        P("grp", "dev", None, None),
        P("grp", "dev", None, None),
        P("grp", "dev", None),
        P("grp", "dev", None),
        P(),
        P("grp", "dev", None),
        P("grp", "dev", None),
        P("grp", "dev", None, None),
        P("grp", "dev", None, None, None),
        P("grp", "dev", None, None),
        P("grp", "dev", None, None),
        P("grp", "dev", None),
        P("grp", "dev", None),
        P(),
        P(),
    )
    out_specs = (
        P("grp", "dev", None, None),
        P("grp", "dev", None, None),
        P("grp", "dev", None, None),
    )
    return jax.shard_map(
        on_device, mesh=mesh, in_specs=in_specs, out_specs=out_specs, check_vma=False
    )
```

profile of v0, /device:TPU:28, one launch (start us, length us, event | category | flops | bytes accessed | tf_op | source)
XLA Modules:
  0.0 153.4 jit_solution(7537027393054033939)
XLA Ops:
  0.6 0.0 copy-start
  0.6 0.7 compare_and_fusion.10
  1.4 0.7 copy.79
  2.2 0.6 copy-done.4
  2.7 1.5 convolution_convert_fusion
  4.3 0.3 copy.86
  4.6 9.2 %gather_fusion.14 = bf16[3072,12]{1,0:T(8,128)(2,1)S(1)} fusion(bf16[12,2048]{0,1:T(8,128)(2,1)S(1)} %copy.86, s32[3072]{0:T(1024)S(1)} %broadcast_clamp_fusion), kind=kCustom, calls=%fused_computation.14 | custom fusion | bytes 159744 | tf_op jit(solution)/shard_map/jit(_take)/gather | solution.py:103
  13.8 0.3 copy.87
  14.1 0.0 copy-start.13
  14.2 0.7 concatenate.32
  14.9 5.1 %all-to-all-start.1 = ((bf16[4,12,12,128]{3,2,1,0:T(8,128)(2,1)}), bf16[4,12,12,128]{3,2,1,0:T(8,128)(2,1)S(1)}, u32[]{:S(2)}, u32[]{:S(2)}) async-start(bf16[4,12,12,128]{3,2,1,0:T(8,128)(2,1)} %concatenate.32), calls=%async_computation.1 | async-start | bytes 393216 | tf_op jit(solution)/shard_map/all_to_all | solution.py:117
  20.0 0.3 copy.76
  20.4 0.2 copy.75
  20.6 0.7 gather_fusion.10
  21.4 0.1 fusion.27
  21.5 0.7 gather_fusion.11
  22.2 0.1 fusion.28
  22.4 0.1 collective-permute-start
  22.4 2.6 %collective-permute-start.1 = (bf16[208,128]{0,1:T(8,128)(2,1)S(1)}, bf16[208,128]{0,1:T(8,128)(2,1)S(1)}, u32[]{:S(2)}, u32[]{:S(2)}) collective-permute-start(bf16[208,128]{0,1:T(8,128)(2,1)S(1)} %get-tuple-element.128), channel_id=1, source_target_pairs={{1,0},{2,1},{3,2},{4,3},{5,4},{6,5},{7,6},{0,7},{9,8},{10,9},{11,1... | collective-permute-start | bytes 159752 | tf_op jit(solution)/shard_map/ppermute | solution.py:17
  25.1 0.6 slice.112
  25.6 0.2 convert_reduce_fusion
  25.8 0.7 pad_add_fusion
  26.6 0.3 reduce-window.16
  26.8 0.1 slice.116
  27.0 0.1 slice_reduce_fusion.1
  27.1 0.1 broadcast_add_fusion
  27.2 7.6 %scatter_custom_fusion = s32[1536]{0:T(1024)S(1)} fusion(s32[1024]{0:T(1024)S(1)} %bitcast.211, s32[1024]{0:T(1024)S(1)} %broadcast.361, s32[]{:T(128)} %constant.145.clone.1), kind=kCustom, calls=%fused_computation.123 | custom fusion | flops 1024 | bytes 6148 | tf_op jit(solution)/shard_map/scatter-add | solution.py:91
  34.8 0.3 reduce-window.24
  35.1 0.1 slice.165
  35.2 0.1 slice_reduce_fusion
  35.3 0.1 add_bitcast_fusion.1
  35.5 5.9 %gather_fusion.12 = s32[1536]{0:T(1024)S(1)} fusion(s32[1024]{0:T(1024)S(1)} %iota.10, s32[2048]{0:T(1024)S(1)} %pad_clamp_fusion.1), kind=kCustom, calls=%fused_computation.12 | custom fusion | bytes 18432 | tf_op jit(solution)/shard_map/jit(_take)/gather | solution.py:91
  41.3 0.7 compare_and_fusion.11
  42.0 0.6 pad_clamp_fusion
  42.7 11.1 %scatter_custom_fusion.4 = f32[1024]{0:T(1024)S(1)} fusion(s32[1536]{0:T(1024)S(1)} %fusion.31, f32[1536]{0:T(1024)S(1)} %reduce.6, f32[]{:T(128)} %constant.151.clone.1), kind=kCustom, calls=%fused_computation.130 | custom fusion | flops 1536 | bytes 4100 | tf_op jit(solution)/shard_map/scatter-add | solution.py:135
  53.8 0.8 maximum_convert_fusion
  54.7 53.5 %conditional.3 = (f32[80,2048]{1,0:T(8,128)S(1)}) conditional(s32[]{:T(128)} %convert_element_type.39, (f32[1,1,2048]{2,1,0:T(1,128)S(1)}, f32[208,512]{0,1:T(8,128)}, f32[80,2048]{0,1:T(8,128)S(1)}, s32[1,1,6,2048]{3,1,2,0:T(1,128)S(1)}) %tuple.77, f32[80,2048]{0,1:T(8,128)S(1)} %bitcast.169), branch_computations={%region_2.5_spmd, %region_3.6_spmd} | conditional | flops 2949120 | bytes 16482312 | solution.py:78
  54.9 0.9 fusion.45
  55.8 0.1 pad_maximum_fusion.1
  55.9 7.6 %gather_fusion.9 = f32[2048,80]{1,0:T(8,128)} fusion(f32[80,2304]{0,1:T(8,128)S(1)} %pad_maximum_fusion.1, s32[2048]{0:T(1024)S(1)} %fusion.17), kind=kCustom, calls=%fused_computation.9.clone | custom fusion | bytes 1318912 | tf_op jit(solution)/shard_map/cond/branch_0_fun/jit(_take)/gather | solution.py:25
  63.5 7.6 %gather_fusion.8 = f32[2048,80]{1,0:T(8,128)} fusion(f32[80,2304]{0,1:T(8,128)S(1)} %pad_maximum_fusion.1, s32[2048]{0:T(1024)S(1)} %fusion.16), kind=kCustom, calls=%fused_computation.8.clone | custom fusion | bytes 1318912 | tf_op jit(solution)/shard_map/cond/branch_0_fun/jit(_take)/gather | solution.py:25
  71.0 7.5 %gather_fusion.7 = f32[2048,80]{1,0:T(8,128)} fusion(f32[80,2304]{0,1:T(8,128)S(1)} %pad_maximum_fusion.1, s32[2048]{0:T(1024)S(1)} %fusion.15), kind=kCustom, calls=%fused_computation.7.clone | custom fusion | bytes 1318912 | tf_op jit(solution)/shard_map/cond/branch_0_fun/jit(_take)/gather | solution.py:25
  78.6 7.5 %gather_fusion.6 = f32[2048,80]{1,0:T(8,128)} fusion(f32[80,2304]{0,1:T(8,128)S(1)} %pad_maximum_fusion.1, s32[2048]{0:T(1024)S(1)} %fusion.14), kind=kCustom, calls=%fused_computation.6.clone | custom fusion | bytes 1318912 | tf_op jit(solution)/shard_map/cond/branch_0_fun/jit(_take)/gather | solution.py:25
  86.1 7.6 %gather_fusion.5 = f32[2048,80]{1,0:T(8,128)} fusion(f32[80,2304]{0,1:T(8,128)S(1)} %pad_maximum_fusion.1, s32[2048]{0:T(1024)S(1)} %fusion.13), kind=kCustom, calls=%fused_computation.5.clone | custom fusion | bytes 1318912 | tf_op jit(solution)/shard_map/cond/branch_0_fun/jit(_take)/gather | solution.py:25
  93.7 7.6 %gather_fusion.4 = f32[2048,80]{1,0:T(8,128)} fusion(f32[80,2304]{0,1:T(8,128)S(1)} %pad_maximum_fusion.1, s32[2048]{0:T(1024)S(1)} %fusion.12), kind=kCustom, calls=%fused_computation.1.clone | custom fusion | bytes 1318912 | tf_op jit(solution)/shard_map/cond/branch_0_fun/jit(_take)/gather | solution.py:23
  101.2 6.6 %fusion.11 = f32[80,2048]{0,1:T(8,128)S(1)} fusion(f32[80,2048]{0,1:T(8,128)S(1)} %get-tuple-element.50, f32[2048,80]{1,0:T(8,128)} %gather_fusion.9, f32[2048,80]{1,0:T(8,128)} %gather_fusion.8, f32[2048,80]{1,0:T(8,128)} %gather_fusion.7, f32[2048,80]{1,0:T(8,128)} %gather_fusion.6, f32[2048,80]{1,0:T(8,128)} %gather_fusion.5, ...), kind=kLoop, calls=%fused_computation.46 | loop fusion | flops 2457600 | bytes 5263360 | tf_op jit(solution)/shard_map/cond/branch_0_fun/add | solution.py:26
  107.8 0.3 copy.91
  108.2 1.0 copy.77
  109.2 0.6 convolution_bitcast_fusion
  109.8 0.2 copy.80
  110.0 2.6 %gather_fusion.13 = f32[1536,24]{1,0:T(8,128)S(1)} fusion(f32[24,1024]{0,1:T(8,128)S(1)} %copy.80, s32[2048]{0:T(1024)S(1)} %copy-done.5), kind=kCustom, calls=%fused_computation.13 | custom fusion | bytes 301056 | tf_op jit(solution)/shard_map/jit(_take)/gather | solution.py:96
  112.6 0.2 copy.81
  112.9 0.8 broadcast_in_dim.114
  113.6 2.2 %scatter_fusion = bf16[4,12,24,128]{3,2,1,0:T(8,128)(2,1)} fusion(bf16[4,12,24,128]{3,2,1,0:T(8,128)(2,1)} %broadcast_in_dim.114, s32[12]{0:T(128)S(1)} %get-tuple-element.132, bf16[12,24,128]{2,1,0:T(8,128)(2,1)S(1)} %fusion.26), kind=kCustom, calls=%fused_computation.17 | custom fusion | bytes 221280 | tf_op jit(solution)/shard_map/scatter | solution.py:110
  115.8 5.1 %all-to-all-start = ((bf16[4,12,24,128]{3,2,1,0:T(8,128)(2,1)}), bf16[4,12,24,128]{3,2,1,0:T(8,128)(2,1)S(1)}, u32[]{:S(2)}, u32[]{:S(2)}) async-start(bf16[4,12,24,128]{3,2,1,0:T(8,128)(2,1)} %scatter_fusion), calls=%async_computation | async-start | bytes 589824 | tf_op jit(solution)/shard_map/all_to_all | solution.py:116
  120.9 0.6 gather_fusion.15
  121.7 0.3 copy.89
  122.0 9.0 %scatter_custom_fusion.3 = f32[12,1024]{0,1:T(8,128)S(1)} fusion(s32[1536]{0:T(1024)} %copy-done.6, f32[1536,12]{1,0:T(8,128)S(1)} %copy.89, f32[]{:T(128)} %constant.151.clone.1), kind=kCustom, calls=%fused_computation.81 | custom fusion | flops 18432 | bytes 49664 | tf_op jit(solution)/shard_map/scatter-add | solution.py:133
  131.0 0.2 multiply_bitcast_fusion
  131.2 0.8 copy.90
  132.0 0.1 copy.82
  132.1 1.6 %copy.83 = f32[3072,24]{1,0:T(8,128)} copy(f32[3072,24]{0,1:T(8,128)S(1)} %bitcast.174) | data formatting | bytes 589824 | tf_op jit(solution)/shard_map/convert_element_type | solution.py:122
  133.8 17.5 %scatter_custom_fusion.2 = f32[24,2048]{0,1:T(8,128)S(1)} fusion(s32[3072]{0:T(1024)} %bitcast.194, f32[3072,24]{1,0:T(8,128)} %copy.83, f32[]{:T(128)} %constant.151.clone.1), kind=kCustom, calls=%fused_computation.77 | custom fusion | flops 73728 | bytes 197120 | tf_op jit(solution)/shard_map/scatter-add | solution.py:123
  151.3 2.1 %fusion.20 = f32[1,1,80,2048]{3,2,1,0:T(8,128)} fusion(f32[80,2048]{1,0:T(8,128)S(1)} %get-tuple-element.100, f32[24,2048]{0,1:T(8,128)S(1)} %scatter_custom_fusion.2, f32[80,24]{0,1:T(8,128)S(1)} %copy-done, f32[]{:T(128)S(6)} %convert_element_type.41), kind=kOutput, calls=%fused_computation.72 | convolution fusion | flops 47513600 | bytes 1515012 | tf_op jit(solution)/shard_map/dot_general | solution.py:124
  (75 shorter events, 0.7 us)
Async XLA Ops:
  0.6 150.6 %copy-start = (f32[80,24]{0,1:T(8,128)S(1)}, f32[80,24]{0,1:T(8,128)}, u32[]{:S(2)}) copy-start(f32[80,24]{0,1:T(8,128)} %param.38) | copy-start | bytes 23044
  2.1 0.6 copy-start.4
  4.6 15.4 %copy-start.1 = (f32[1,1,80,2048]{3,2,1,0:T(8,128)S(1)}, f32[1,1,80,2048]{3,2,1,0:T(8,128)}, u32[]{:S(2)}) copy-start(f32[1,1,80,2048]{3,2,1,0:T(8,128)} %param.34) | copy-start | bytes 1966084
  14.1 6.2 %copy-start.13 = (s32[1,1,256]{2,1,0:T(1,128)S(1)}, s32[1,1,256]{2,1,0:T(1,128)}, u32[]{:S(2)}) copy-start(s32[1,1,256]{2,1,0:T(1,128)} %param.36) | copy-start | bytes 3076
  14.1 6.2 %copy-start.14 = (s32[1,1,256]{2,1,0:T(1,128)S(1)}, s32[1,1,256]{2,1,0:T(1,128)}, u32[]{:S(2)}) copy-start(s32[1,1,256]{2,1,0:T(1,128)} %param.27) | copy-start | bytes 3076
  14.1 6.2 %copy-start.2 = (f32[1,1,128,1024]{3,2,1,0:T(8,128)S(1)}, f32[1,1,128,1024]{3,2,1,0:T(8,128)}, u32[]{:S(2)}) copy-start(f32[1,1,128,1024]{3,2,1,0:T(8,128)} %param.25) | copy-start | bytes 1572868
  14.9 100.9 %all-to-all-start.1 = ((bf16[4,12,12,128]{3,2,1,0:T(8,128)(2,1)}), bf16[4,12,12,128]{3,2,1,0:T(8,128)(2,1)S(1)}, u32[]{:S(2)}, u32[]{:S(2)}) async-start(bf16[4,12,12,128]{3,2,1,0:T(8,128)(2,1)} %concatenate.32), calls=%async_computation.1 | async-start | bytes 393216 | tf_op jit(solution)/shard_map/all_to_all | solution.py:117
  20.4 4.7 %copy-start.12 = (s32[1,1,1024]{2,1,0:T(1,128)S(1)}, s32[1,1,1024]{2,1,0:T(1,128)}, u32[]{:S(2)}) copy-start(s32[1,1,1024]{2,1,0:T(1,128)} %param.30) | copy-start | bytes 12292
  20.4 5.2 %copy-start.15 = (s32[1,1,12,1]{2,3,1,0:T(1,128)S(1)}, s32[1,1,12,1]{2,3,1,0:T(1,128)}, u32[]{:S(2)}) copy-start(s32[1,1,12,1]{2,3,1,0:T(1,128)} %param.32) | copy-start | bytes 148
  22.4 31.5 %collective-permute-start = (bf16[208,128]{0,1:T(8,128)(2,1)S(1)}, bf16[208,128]{0,1:T(8,128)(2,1)S(1)}, u32[]{:S(2)}, u32[]{:S(2)}) collective-permute-start(bf16[208,128]{0,1:T(8,128)(2,1)S(1)} %get-tuple-element.127), channel_id=1, source_target_pairs={{0,1},{1,2},{2,3},{3,4},{4,5},{5,6},{6,7},{7,0},{8,9},{9,10},{10,1... | collective-permute-start | bytes 159752 | tf_op jit(solution)/shard_map/ppermute | solution.py:16
  22.4 31.4 %collective-permute-start.1 = (bf16[208,128]{0,1:T(8,128)(2,1)S(1)}, bf16[208,128]{0,1:T(8,128)(2,1)S(1)}, u32[]{:S(2)}, u32[]{:S(2)}) collective-permute-start(bf16[208,128]{0,1:T(8,128)(2,1)S(1)} %get-tuple-element.128), channel_id=1, source_target_pairs={{1,0},{2,1},{3,2},{4,3},{5,4},{6,5},{7,6},{0,7},{9,8},{10,9},{11,1... | collective-permute-start | bytes 159752 | tf_op jit(solution)/shard_map/ppermute | solution.py:17
  35.4 7.2 %copy-start.10 = (f32[1,1,1536]{2,1,0:T(1,128)S(1)}, f32[1,1,1536]{2,1,0:T(1,128)}, u32[]{:S(2)}) copy-start(f32[1,1,1536]{2,1,0:T(1,128)} %param.31) | copy-start | bytes 18436
  35.4 19.2 %copy-start.3 = (s32[1,1,6,2048]{3,1,2,0:T(1,128)S(1)}, s32[1,1,6,2048]{3,1,2,0:T(1,128)}, u32[]{:S(2)}) copy-start(s32[1,1,6,2048]{3,1,2,0:T(1,128)} %param.35) | copy-start | bytes 147460
  35.5 19.2 %copy-start.9 = (f32[1,1,2048]{2,1,0:T(1,128)S(1)}, f32[1,1,2048]{2,1,0:T(1,128)}, u32[]{:S(2)}) copy-start(f32[1,1,2048]{2,1,0:T(1,128)} %param.37) | copy-start | bytes 24580
  42.0 12.7 %copy-start.6 = (s32[1536]{0:T(1024)}, s32[1536]{0:T(1024)S(1)}, u32[]{:S(2)}) copy-start(s32[1536]{0:T(1024)S(1)} %fusion.31) | copy-start | bytes 18436
  108.2 1.0 copy-start.7
  108.2 1.8 %copy-start.5 = (s32[2048]{0:T(1024)S(1)}, s32[2048]{0:T(1024)}, u32[]{:S(2)}) copy-start(s32[2048]{0:T(1024)} %pad_clamp_fusion) | copy-start | bytes 24580
  110.0 2.8 %copy-start.8 = (pred[12,128]{1,0:T(8,128)(4,1)S(1)}, pred[12,128]{1,0:T(8,128)(4,1)}, u32[]{:S(2)}) copy-start(pred[12,128]{1,0:T(8,128)(4,1)} %compare_and_fusion.11) | copy-start | bytes 4612
  115.8 16.2 %all-to-all-start = ((bf16[4,12,24,128]{3,2,1,0:T(8,128)(2,1)}), bf16[4,12,24,128]{3,2,1,0:T(8,128)(2,1)S(1)}, u32[]{:S(2)}, u32[]{:S(2)}) async-start(bf16[4,12,24,128]{3,2,1,0:T(8,128)(2,1)} %scatter_fusion), calls=%async_computation | async-start | bytes 589824 | tf_op jit(solution)/shard_map/all_to_all | solution.py:116
where the time goes:
time: 155 us; the launch traced here: 153 us
  local copies, waits for them, and re-layouts  77.9 us (50%)
  other arithmetic  57.2 us (37%)
  starting transfers between devices  12.9 us (8%)
  matrix products  4.23 us (3%)
    gather x5, local copies, waits for them, and re-layouts, stencil(): total = total + jnp.take(pool, neighbours[which], axis=1)  37.8 us
    scatter-add x1, other arithmetic, on_device(): jnp.zeros((fields, cells), jnp.float32).at[:, cell_index].add(incoming)  17.5 us
    scatter-add x1, other arithmetic, on_device(): weight_sum = jnp.zeros((columns,), jnp.float32).at[column].add(weights)  11.1 us
    gather x2, local copies, waits for them, and re-layouts, on_device(): jnp.take(returned, cell_index, axis=1)  9.51 us
    scatter-add x1, other arithmetic, on_device(): jnp.zeros((ret_fields, columns), jnp.float32).at[:, column]  9 us
    scatter-add x1, other arithmetic, on_device(): jnp.repeat(jnp.arange(columns, dtype=jnp.int32), margin_counts[0, 0], tot...  7.62 us
    gather x1, local copies, waits for them, and re-layouts, stencil(): total = jnp.take(pool, neighbours[0], axis=1)  7.55 us
    add x1, other arithmetic, stencil(): return state + mixing[None, :] * (total / neighbours.shape[0] - state)  6.58 us
  transfers between devices with their start and end apart: 4, of which 0 were waited for; matrix products, arithmetic and copies ran while one was open for 68% of the time, Pallas kernels for 0%

commit v1 on v0

v1 whole, which is shorter than its diff:
```python
import functools

import jax
import jax.numpy as jnp
from jax import lax
from jax.experimental import pallas as pl
from jax.experimental.pallas import tpu as pltpu
from jax.sharding import PartitionSpec as P

EXACT = lax.Precision.HIGHEST
BF = jnp.bfloat16
F32 = jnp.float32
NT = (((1,), (1,)), ((), ()))


def split(x):
    hi = x.astype(BF)
    return hi, (x - hi.astype(F32)).astype(BF)


def mm(a, b):
    return jnp.dot(a, b, preferred_element_type=F32)


def one_hot(idx, rows, base):
    width = idx.shape[1]
    place = lax.broadcasted_iota(jnp.int32, (rows, width), 0) + base
    return jnp.where(place == idx, 1.0, 0.0).astype(BF)


def counts_matrix(out_ref, high_ref, idx_rows, base, at):
    width = idx_rows[0].shape[1]
    highs = out_ref.shape[0] // base
    bits = base.bit_length() - 1
    low = [i & (base - 1) for i in idx_rows]
    for k, i in enumerate(idx_rows):
        high = jnp.broadcast_to(i >> bits, (16, width))
        for h in range(highs):
            high_ref[k * highs + h, :, :width] = jnp.where(high == h, 1.0, 0.0).astype(BF)
    for t in range(base // 16):
        parts = [one_hot(i, 16, t * 16) for i in low]
        for h in range(highs):
            total = parts[0] * high_ref[h, :, :width]
            for k in range(1, len(parts)):
                total = total + parts[k] * high_ref[k * highs + h, :, :width]
            out_ref[pl.ds(h * base + t * 16, 16), at] = total


def base_of(length):
    return 256 if length % 256 == 0 else 128


def kernel(
    sizes,
    air_ref, anbr_ref, asend_ref, amix_ref, fw_ref, counts_ref, mw_ref, owner_ref,
    recv_ref, sea_ref, onbr_ref, osend_ref, omix_ref, force_ref, retw_ref,
    air_out, sea_out, back_out,
    pack, halo, apool, opool, amat, omat, member, cellmat, high,
    rows, up_out, up_in, down_out, down_in, retw, slab, ret_bf,
    halo_send, halo_recv, x_send, x_recv,
):
    groups, devs, air_groups = sizes
    sea_groups = groups - air_groups
    g, d = lax.axis_index("grp"), lax.axis_index("dev")
    lower, upper = lax.rem(d + devs - 1, devs), lax.rem(d + 1, devs)
    is_air = g < air_groups
    half = halo.shape[2]
    capacity, block = recv_ref.shape[3], recv_ref.shape[4]
    span = capacity * block
    levels_a, columns = air_ref.shape[2:]
    levels_o, cells = sea_ref.shape[2:]
    fields = fw_ref.shape[0]
    ret_fields = retw_ref.shape[0]
    ret_pad = retw.shape[0]
    blocks = owner_ref.shape[2]
    first = jnp.where(is_air, air_groups, 0)
    mine = jnp.where(is_air, g, g - air_groups)
    partners = air_groups

    barrier = pltpu.get_barrier_semaphore()
    pl.semaphore_signal(barrier, inc=1, device_id={"dev": lower})
    pl.semaphore_signal(barrier, inc=1, device_id={"dev": upper})
    for p in range(partners):
        pl.semaphore_signal(barrier, inc=1, device_id={"grp": first + p})

    def packed(state_ref, send_ref, pool):
        levels, length = state_ref.shape[2:]
        top, rest = split(state_ref[0, 0])
        pool[:levels, :length] = top
        pool[levels:, :length] = rest
        picker = one_hot(send_ref[0], length, 0)
        chosen = mm(top, picker).astype(BF)
        pack[0, :levels, :] = chosen[:, :half]
        pack[1, :levels, :] = chosen[:, half:]
        if levels < pack.shape[1]:
            pack[:, levels:, :] = jnp.zeros((2, pack.shape[1] - levels, half), BF)

    @pl.when(is_air)
    def _():
        packed(air_ref, asend_ref, apool)

    @pl.when(jnp.logical_not(is_air))
    def _():
        packed(sea_ref, osend_ref, opool)

    pl.semaphore_wait(barrier, 2 + partners)
    to_upper = pltpu.make_async_remote_copy(
        src_ref=pack.at[1], dst_ref=halo.at[0], send_sem=halo_send.at[0],
        recv_sem=halo_recv.at[0], device_id={"dev": upper})
    to_lower = pltpu.make_async_remote_copy(
        src_ref=pack.at[0], dst_ref=halo.at[1], send_sem=halo_send.at[1],
        recv_sem=halo_recv.at[1], device_id={"dev": lower})
    to_upper.start()
    to_lower.start()

    up = [
        pltpu.make_async_remote_copy(
            src_ref=up_out.at[p], dst_ref=up_in.at[mine], send_sem=x_send.at[p],
            recv_sem=x_recv.at[mine], device_id={"grp": first + p})
        for p in range(partners)
    ]
    down = [
        pltpu.make_async_remote_copy(
            src_ref=down_out.at[p], dst_ref=down_in.at[mine], send_sem=x_send.at[p],
            recv_sem=x_recv.at[mine], device_id={"grp": first + p})
        for p in range(partners)
    ]

    def take_halo(pool, levels, length):
        to_upper.wait()
        to_lower.wait()
        for side in range(2):
            at = slice(length + side * half, length + (side + 1) * half)
            pool[:levels, at] = halo[side, :levels, :]
            pool[levels:, at] = jnp.zeros((levels, half), BF)

    @pl.when(is_air)
    def _():
        sea_out[0, 0] = sea_ref[0, 0]
        neighbours = anbr_ref.shape[2]
        base = base_of(amat.shape[0])
        width = high.shape[2]

        def build(c, _):
            at = pl.ds(pl.multiple_of(c * width, width), width)
            rows_in = [anbr_ref[0, 0, k : k + 1, at] for k in range(neighbours)]
            counts_matrix(amat, high, rows_in, base, at)
            return _

        lax.fori_loop(0, columns // width, build, 0)

        cnt = jnp.broadcast_to(counts_ref[0].astype(F32), (128, columns)).astype(BF)
        row_count = mw_ref.shape[2]

        def build_member(c, _):
            shape = (128, columns)
            a = lax.broadcasted_iota(jnp.int32, shape, 0) + c * 128
            b = lax.broadcasted_iota(jnp.int32, shape, 1)
            upto = jnp.where(b <= a, 1.0, 0.0).astype(BF)
            before = jnp.where(b < a, 1.0, 0.0).astype(BF)
            end = lax.dot_general(upto, cnt, NT, preferred_element_type=F32)
            start = lax.dot_general(before, cnt, NT, preferred_element_type=F32)
            for r in range(row_count // 128):
                at = lax.broadcasted_iota(jnp.int32, (128, 128), 1).astype(F32) + r * 128.0
                inside = (at >= start) & (at < end)
                member[pl.ds(pl.multiple_of(c * 128, 128), 128), r * 128 : (r + 1) * 128] = (
                    jnp.where(inside, 1.0, 0.0).astype(BF))
            return _

        lax.fori_loop(0, columns // 128, build_member, 0)
        take_halo(apool, levels_a, columns)

        def sweep(c, _):
            at = pl.ds(pl.multiple_of(c * width, width), width)
            both = mm(apool[...], amat[:, at])
            mean = (both[:levels_a] + both[levels_a:]) * (1.0 / neighbours)
            state = air_ref[0, 0, :, at]
            new = state + amix_ref[0, :, at] * (mean - state)
            air_out[0, 0, :, at] = new
            flux = jnp.dot(fw_ref[...], new, precision=EXACT, preferred_element_type=F32)
            top, rest = split(flux)
            slab[:fields, at] = top
            slab[fields : 2 * fields, at] = rest
            return _

        lax.fori_loop(0, columns // width, sweep, 0)
        for b in range(blocks):
            at = slice(b * block, (b + 1) * block)
            both = mm(slab[: 2 * fields, :columns], member[:, at])
            weight = mw_ref[0, :, at]
            rows[b] = (both[:fields] + both[fields:]) * weight
        owner = [owner_ref[0, 0, b, 0] for b in range(blocks)]
        slot = []
        for b in range(blocks):
            s = jnp.int32(0)
            for e in range(b):
                s = s + jnp.where(owner[e] == owner[b], 1, 0)
            slot.append(s)
        place = [owner[b] * capacity + slot[b] for b in range(blocks)]
        for o in range(sea_groups):
            for k in range(capacity):
                source = jnp.int32(0)
                valid = jnp.int32(0)
                for b in range(blocks):
                    hit = place[b] == o * capacity + k
                    source = jnp.where(hit, b, source)
                    valid = jnp.where(hit, 1, valid)
                value = rows[source] * valid.astype(F32)
                up_out[o, :, k * block : (k + 1) * block] = value.astype(BF)
            up[o].start()
        for p in range(partners):
            pltpu.make_async_remote_copy(
                src_ref=down_out.at[p], dst_ref=down_in.at[p], send_sem=x_send.at[p],
                recv_sem=x_recv.at[p], device_id={"grp": first + p}).wait_recv()
        for b in range(blocks):
            at = slice(b * block, (b + 1) * block)
            weight = jnp.broadcast_to(mw_ref[0, :, at], (ret_pad, block))
            value = down_in[owner[b], slot[b]].astype(F32) * weight
            top, rest = split(value)
            wtop, wrest = split(weight)
            for i, part in enumerate((top, rest, wtop, wrest)):
                slab[i * ret_pad : (i + 1) * ret_pad, at] = part
        depth = 4 * ret_pad
        r0 = lax.broadcasted_iota(jnp.int32, (2 * ret_pad, depth), 0)
        c0 = lax.broadcasted_iota(jnp.int32, (2 * ret_pad, depth), 1)
        near = jnp.where(r0 < ret_pad, r0, r0 + ret_pad)
        pick = jnp.where((c0 == near) | (c0 == near + ret_pad), 1.0, 0.0)

        sums = lax.dot_general(
            member[...], slab[:depth, :row_count], NT, preferred_element_type=F32)
        both = lax.dot_general(pick, sums, NT, precision=EXACT, preferred_element_type=F32)
        back_out[0, 0] = (both[:ret_pad] / both[ret_pad:])[:ret_fields]
        for p in range(partners):
            up[p].wait_send()

    @pl.when(jnp.logical_not(is_air))
    def _():
        air_out[0, 0] = air_ref[0, 0]
        back_out[0, 0] = jnp.zeros(back_out.shape[2:], F32)
        neighbours = onbr_ref.shape[2]
        width = high.shape[2]
        retw[...] = jnp.zeros(retw.shape, F32)
        retw[:ret_fields] = retw_ref[...]
        ret_bf[...] = jnp.dot(
            retw[...], sea_ref[0, 0], precision=EXACT, preferred_element_type=F32).astype(BF)
        base = base_of(cells)
        for s in range(air_groups):

            def build(k, _):
                at = pl.ds(pl.multiple_of(s * span + k * 2 * block, 2 * block), 2 * block)
                idx = jnp.concatenate(
                    [recv_ref[0, 0, s, pl.ds(2 * k + i, 1), :] for i in range(2)], axis=1)
                counts_matrix(cellmat, high, [idx], base, at)
                looked = mm(ret_bf[...], cellmat[:, at]).astype(BF)
                for i in range(2):
                    down_out[s, 2 * k + i] = looked[:, i * block : (i + 1) * block]
                return _

            lax.fori_loop(0, capacity // 2, build, 0)
            down[s].start()
        take_halo(opool, levels_o, cells)
        base_p = base_of(omat.shape[0])

        def sweep(c, _):
            at = pl.ds(pl.multiple_of(c * width, width), width)
            rows_in = [onbr_ref[0, 0, k : k + 1, at] for k in range(neighbours)]
            counts_matrix(omat, high, rows_in, base_p, slice(0, width))
            both = mm(opool[...], omat[...])
            mean = (both[:levels_o] + both[levels_o:]) * (1.0 / neighbours)
            state = sea_ref[0, 0, :, at]
            sea_out[0, 0, :, at] = state + omix_ref[0, :, at] * (mean - state)
            return _

        lax.fori_loop(0, cells // width, sweep, 0)
        for p in range(partners):
            pltpu.make_async_remote_copy(
                src_ref=up_out.at[p], dst_ref=up_in.at[p], send_sem=x_send.at[p],
                recv_sem=x_recv.at[p], device_id={"grp": first + p}).wait_recv()
        tall = min(cells, 512)

        def force(c, _):
            at = pl.ds(pl.multiple_of(c * tall, tall), tall)
            flux = jnp.zeros((tall, fields), F32)
            for s in range(air_groups):
                flux = flux + lax.dot_general(
                    cellmat[at, s * span : (s + 1) * span], up_in[s], NT,
                    preferred_element_type=F32)
            sea_out[0, 0, :, at] += lax.dot_general(
                force_ref[...], flux, NT, precision=EXACT, preferred_element_type=F32)
            return _

        lax.fori_loop(0, cells // tall, force, 0)
        for p in range(partners):
            down[p].wait_send()


def solution(mesh):
    groups, devs = mesh.shape["grp"], mesh.shape["dev"]
    in_specs = (
        P("grp", "dev", None, None), P("grp", "dev", None, None), P("grp", "dev", None),
        P("grp", "dev", None), P(), P("grp", "dev", None), P("grp", "dev", None),
        P("grp", "dev", None, None), P("grp", "dev", None, None, None),
        P("grp", "dev", None, None), P("grp", "dev", None, None), P("grp", "dev", None),
        P("grp", "dev", None), P(), P(),
    )
    out_specs = (P("grp", "dev", None, None),) * 3

    def on_device(*args):
        air, anbr, asend, _, fw, _, mw, owner, recv, sea, onbr, _, _, _, ret = args
        levels_a, columns = air.shape[2:]
        levels_o, cells = sea.shape[2:]
        half = asend.shape[2] // 2
        air_groups, capacity, block = recv.shape[2:]
        sea_groups = groups - air_groups
        fields, ret_fields = fw.shape[0], ret.shape[0]
        ret_pad = -(-ret_fields // 16) * 16
        row_count = mw.shape[2]
        pool_a, pool_o = columns + 2 * half, cells + 2 * half
        width = 256
        deep = max(
            anbr.shape[2] * (pool_a // base_of(pool_a)),
            onbr.shape[2] * (pool_o // base_of(pool_o)),
            cells // base_of(cells),
        )
        vmem = pl.BlockSpec(memory_space=pltpu.VMEM)
        smem = pl.BlockSpec(memory_space=pltpu.SMEM)
        ins = [vmem] * 15
        ins[7] = smem
        levels = max(levels_a, levels_o)
        V = pltpu.VMEM
        scratch = [
            V((2, levels, half), BF), V((2, levels, half), BF),
            V((2 * levels_a, pool_a), BF), V((2 * levels_o, pool_o), BF),
            V((pool_a, columns), BF), V((pool_o, width), BF),
            V((columns, row_count), BF), V((cells, air_groups * capacity * block), BF),
            V((deep, 16, width), BF),
            V((owner.shape[2], fields, block), F32),
            V((sea_groups, fields, capacity * block), BF),
            V((air_groups, fields, capacity * block), BF),
            V((air_groups, capacity, ret_pad, block), BF),
            V((sea_groups, capacity, ret_pad, block), BF),
            V((ret_pad, levels_o), F32),
            V((max(4 * ret_pad, 2 * fields), max(row_count, columns)), BF),
            V((ret_pad, cells), BF),
            pltpu.SemaphoreType.DMA((2,)), pltpu.SemaphoreType.DMA((2,)),
            pltpu.SemaphoreType.DMA((air_groups,)), pltpu.SemaphoreType.DMA((air_groups,)),
        ]
        return pl.pallas_call(
            functools.partial(kernel, (groups, devs, air_groups)),
            out_shape=(
                jax.ShapeDtypeStruct(air.shape, F32),
                jax.ShapeDtypeStruct(sea.shape, F32),
                jax.ShapeDtypeStruct((1, 1, ret_fields, columns), F32),
            ),
            in_specs=ins,
            out_specs=(vmem,) * 3,
            scratch_shapes=scratch,
            compiler_params=pltpu.CompilerParams(
                collective_id=0, has_side_effects=True, vmem_limit_bytes=60 * 1024 * 1024),
            name="couple",
        )(*args)

    return jax.shard_map(
        on_device, mesh=mesh, in_specs=in_specs, out_specs=out_specs, check_vma=False)
```

time: 155 us -> 36.2 us (0.23)
  local copies, waits for them, and re-layouts: 77.9 us -> 9.01 us
  other arithmetic: 57.2 us -> 0 us
  Pallas kernels: 0 us -> 26.1 us
  starting transfers between devices: 12.9 us -> 0 us
  matrix products: 4.23 us -> 0 us
    gather x14 -> x0, local copies, waits for them, and re-layouts: 65.7 us -> none  [the longest x5 37.8 us: stencil(): total = total + jnp.take(pool, neighbours[which], axis=1)]
    scatter-add x4 -> x0, other arithmetic: 45.2 us -> none  [the longest x1 17.5 us: on_device(): jnp.zeros((fields, cells), jnp.float32).at[:, cell_index].add(incoming)]
    pallas_call x0 -> x1, Pallas kernels: none -> 26.1 us  [on_device(): pl.pallas_call(functools.partial(kernel, (groups, devs, air_groups)), out...]
    all_to_all x2 -> x0, starting transfers between devices: 10.2 us -> none  [the longest x1 5.09 us: on_device(): lax.all_to_all(upward, 'grp', split_axis=0, concat_axis=0, tiled=True)]
    add x1 -> x0, other arithmetic: 6.58 us -> none  [stencil(): return state + mixing[None, :] * (total / neighbours.shape[0] - state)]
    unnamed x36 -> x10, local copies, waits for them, and re-layouts: 2.75 us -> 7.44 us
    dot_general x3 -> x0, matrix products: 4.23 us -> none  [the longest x1 2.15 us: on_device(): forcing = jnp.dot(force_weight, cell_flux, precision=EXACT_DOT)]
    ppermute x2 -> x0, starting transfers between devices: 2.69 us -> none  [the longest x1 2.63 us: extended_2(): after = lax.ppermute(leading, axis, down)]
  transfers between devices with their start and end apart: 4 -> 0, of which waited for: 0 -> 0; matrix products, arithmetic and copies ran while one was open for 68% -> 0% of each run, Pallas kernels for 0% -> 0%
where the time goes in v1:
time: 36.2 us; the launch traced here: 35.8 us
  Pallas kernels  26.1 us (72%)
  local copies, waits for them, and re-layouts  9.01 us (25%)
  between operations  0.66 us (2%)
    pallas_call x1, Pallas kernels, on_device(): pl.pallas_call(functools.partial(kernel, (groups, devs, air_groups)), out...  26.1 us
    unnamed x10, local copies, waits for them, and re-layouts  7.44 us
    pallas_call x1, local copies, waits for them, and re-layouts, on_device(): pl.pallas_call(functools.partial(kernel, (groups, devs, air_groups)), out...  1.57 us

profile of v1, /device:TPU:28, one launch (start us, length us, event | category | flops | bytes accessed | tf_op | source)
XLA Modules:
  0.0 35.8 jit_solution(4879477305176226240)
XLA Ops:
  0.6 0.0 copy-start.1
  0.6 1.3 %copy.18.owner_ref = s32[1,1,12,1]{3,2,1,0:T(8,128)} copy(s32[1,1,12,1]{2,3,1,0:T(1,128)} %param.22) | data formatting | bytes 96 | tf_op args[7]
  2.0 1.3 %copy.19.recv_ref = s32[1,1,2,12,128]{4,3,2,1,0:T(8,128)} copy(s32[1,1,2,12,128]{4,2,3,1,0:T(2,128)} %param.23) | data formatting | bytes 24576 | tf_op args[8]
  3.3 1.4 %copy.21.force_ref = f32[80,24]{1,0:T(8,128)} copy(f32[80,24]{0,1:T(8,128)} %param.28) | data formatting | bytes 15360 | tf_op args[13]
  4.7 0.0 copy-done.1
  4.7 0.6 %copy.20.onbr_ref = s32[1,1,6,2048]{3,2,1,0:T(8,128)} copy(s32[1,1,6,2048]{3,1,2,0:T(1,128)S(1)} %copy-done.1) | data formatting | bytes 98304 | tf_op args[10]
  5.4 26.1 %couple.1 = (f32[1,1,128,1024]{3,2,1,0:T(8,128)}, f32[1,1,80,2048]{3,2,1,0:T(8,128)}, f32[1,1,12,1024]{3,2,1,0:T(8,128)}) custom-call(f32[1,1,128,1024]{3,2,1,0:T(8,128)} %air_ref.1, s32[1,1,4,1024]{3,2,1,0:T(4,128)} %anbr_ref.1, s32[1,1,256]{2,1,0:T(1,128)} %asend_ref.1, f32[1,1,1024]{2,1,0:T(1,128)} %amix_ref.1, f32[24,128]{1,0:T(8,128)} %fw_ref.1, ...), custom_call_target="tpu_custom_call" | custom-call | tf_op jit(solution)/shard_map/couple/pallas_call | solution.py:348
  31.5 0.0 copy-start
  31.5 1.6 %copy.22 = f32[1,1,12,1024]{3,1,2,0:T(1,128)} copy(f32[1,1,12,1024]{3,2,1,0:T(8,128)} %get-tuple-element.5) | data formatting | bytes 98304 | tf_op jit(solution)/shard_map/couple/pallas_call | solution.py:348
  33.1 1.9 %copy.25 = f32[1,1,128,1024]{3,2,1,0:T(8,128)} copy(f32[1,1,128,1024]{3,2,1,0:T(8,128)} %get-tuple-element.9) | data formatting | bytes 1048576
  35.0 0.0 copy-done
  35.0 0.8 %copy.26 = f32[1,1,80,2048]{3,2,1,0:T(8,128)} copy(f32[1,1,80,2048]{3,2,1,0:T(8,128)S(1)} %copy-done) | data formatting | bytes 1310720
Async XLA Ops:
  0.6 4.1 %copy-start.1 = (s32[1,1,6,2048]{3,1,2,0:T(1,128)S(1)}, s32[1,1,6,2048]{3,1,2,0:T(1,128)}, u32[]{:S(2)}) copy-start(s32[1,1,6,2048]{3,1,2,0:T(1,128)} %param.25) | copy-start | bytes 147460
  31.5 3.5 %copy-start = (f32[1,1,80,2048]{3,2,1,0:T(8,128)S(1)}, f32[1,1,80,2048]{3,2,1,0:T(8,128)}, u32[]{:S(2)}) copy-start(f32[1,1,80,2048]{3,2,1,0:T(8,128)} %get-tuple-element.10) | copy-start | bytes 1966084

commit v2 on v1

--- a/solution.py
+++ b/solution.py
@@ -22,6 +22,15 @@
     return jnp.dot(a, b, preferred_element_type=F32)
 
 
+def low_hot(low, t):
+    place = lax.broadcasted_iota(jnp.int32, low.shape, 0).astype(F32).astype(BF)
+    return jnp.where(low - jnp.asarray(16.0 * t, BF) == place, jnp.asarray(1, BF), jnp.asarray(0, BF))
+
+
+def as_rows(idx, rows):
+    return jnp.broadcast_to(idx.astype(F32), (rows, idx.shape[1])).astype(BF)
+
+
 def one_hot(idx, rows, base):
     width = idx.shape[1]
     place = lax.broadcasted_iota(jnp.int32, (rows, width), 0) + base
@@ -32,13 +41,13 @@
     width = idx_rows[0].shape[1]
     highs = out_ref.shape[0] // base
     bits = base.bit_length() - 1
-    low = [i & (base - 1) for i in idx_rows]
+    low = [as_rows(i & (base - 1), 16) for i in idx_rows]
     for k, i in enumerate(idx_rows):
         high = jnp.broadcast_to(i >> bits, (16, width))
         for h in range(highs):
             high_ref[k * highs + h, :, :width] = jnp.where(high == h, 1.0, 0.0).astype(BF)
     for t in range(base // 16):
-        parts = [one_hot(i, 16, t * 16) for i in low]
+        parts = [low_hot(i, t) for i in low]
         for h in range(highs):
             total = parts[0] * high_ref[h, :, :width]
             for k in range(1, len(parts)):
@@ -55,7 +64,7 @@
     air_ref, anbr_ref, asend_ref, amix_ref, fw_ref, counts_ref, mw_ref, owner_ref,
     recv_ref, sea_ref, onbr_ref, osend_ref, omix_ref, force_ref, retw_ref,
     air_out, sea_out, back_out,
-    pack, halo, apool, opool, amat, omat, member, cellmat, high,
+    pack, halo, apool, opool, amat, omat0, omat1, member, lowmat, spread, high, high1,
     rows, up_out, up_in, down_out, down_in, retw, slab, ret_bf,
     halo_send, halo_recv, x_send, x_recv,
 ):
@@ -65,14 +74,15 @@
     lower, upper = lax.rem(d + devs - 1, devs), lax.rem(d + 1, devs)
     is_air = g < air_groups
     half = halo.shape[2]
-    capacity, block = recv_ref.shape[3], recv_ref.shape[4]
+    capacity, block = recv_ref.shape[2], recv_ref.shape[4]
     span = capacity * block
     levels_a, columns = air_ref.shape[2:]
     levels_o, cells = sea_ref.shape[2:]
     fields = fw_ref.shape[0]
+    field_pad = spread.shape[0] // (cells // lowmat.shape[0])
     ret_fields = retw_ref.shape[0]
     ret_pad = retw.shape[0]
-    blocks = owner_ref.shape[2]
+    blocks = owner_ref.shape[3]
     first = jnp.where(is_air, air_groups, 0)
     mine = jnp.where(is_air, g, g - air_groups)
     partners = air_groups
@@ -85,9 +95,8 @@
 
     def packed(state_ref, send_ref, pool):
         levels, length = state_ref.shape[2:]
-        top, rest = split(state_ref[0, 0])
-        pool[:levels, :length] = top
-        pool[levels:, :length] = rest
+        top = state_ref[0, 0].astype(BF)
+        pool[:, :length] = top
         picker = one_hot(send_ref[0], length, 0)
         chosen = mm(top, picker).astype(BF)
         pack[0, :levels, :] = chosen[:, :half]
@@ -131,8 +140,7 @@
         to_lower.wait()
         for side in range(2):
             at = slice(length + side * half, length + (side + 1) * half)
-            pool[:levels, at] = halo[side, :levels, :]
-            pool[levels:, at] = jnp.zeros((levels, half), BF)
+            pool[:, at] = halo[side, :levels, :]
 
     @pl.when(is_air)
     def _():
@@ -170,10 +178,9 @@
         lax.fori_loop(0, columns // 128, build_member, 0)
         take_halo(apool, levels_a, columns)
 
-        def sweep(c, _):
-            at = pl.ds(pl.multiple_of(c * width, width), width)
-            both = mm(apool[...], amat[:, at])
-            mean = (both[:levels_a] + both[levels_a:]) * (1.0 / neighbours)
+        for c in range(columns // width):
+            at = slice(c * width, (c + 1) * width)
+            mean = mm(apool[...], amat[:, at]) * (1.0 / neighbours)
             state = air_ref[0, 0, :, at]
             new = state + amix_ref[0, :, at] * (mean - state)
             air_out[0, 0, :, at] = new
@@ -181,15 +188,11 @@
             top, rest = split(flux)
             slab[:fields, at] = top
             slab[fields : 2 * fields, at] = rest
-            return _
-
-        lax.fori_loop(0, columns // width, sweep, 0)
+        both = mm(slab[: 2 * fields, :columns], member[...])
+        values = (both[:fields] + both[fields:]) * mw_ref[0]
         for b in range(blocks):
-            at = slice(b * block, (b + 1) * block)
-            both = mm(slab[: 2 * fields, :columns], member[:, at])
-            weight = mw_ref[0, :, at]
-            rows[b] = (both[:fields] + both[fields:]) * weight
-        owner = [owner_ref[0, 0, b, 0] for b in range(blocks)]
+            rows[b] = values[:, b * block : (b + 1) * block]
+        owner = [owner_ref[0, 0, 0, b] for b in range(blocks)]
         slot = []
         for b in range(blocks):
             s = jnp.int32(0)
@@ -229,67 +232,93 @@
         sums = lax.dot_general(
             member[...], slab[:depth, :row_count], NT, preferred_element_type=F32)
         both = lax.dot_general(pick, sums, NT, precision=EXACT, preferred_element_type=F32)
-        back_out[0, 0] = (both[:ret_pad] / both[ret_pad:])[:ret_fields]
+        ratio = both[:ret_pad] / both[ret_pad:]
+        for f in range(ret_fields):
+            back_out[0, f] = ratio[f : f + 1]
         for p in range(partners):
             up[p].wait_send()
 
     @pl.when(jnp.logical_not(is_air))
     def _():
         air_out[0, 0] = air_ref[0, 0]
-        back_out[0, 0] = jnp.zeros(back_out.shape[2:], F32)
-        neighbours = onbr_ref.shape[2]
+        back_out[...] = jnp.zeros(back_out.shape, F32)
+        neighbours = onbr_ref.shape[1]
         width = high.shape[2]
+        base = lowmat.shape[0]
+        bits = base.bit_length() - 1
+        highs = cells // base
         retw[...] = jnp.zeros(retw.shape, F32)
         retw[:ret_fields] = retw_ref[...]
-        ret_bf[...] = jnp.dot(
+        returned = jnp.dot(
             retw[...], sea_ref[0, 0], precision=EXACT, preferred_element_type=F32).astype(BF)
-        base = base_of(cells)
+        for h in range(highs):
+            ret_bf[h * ret_pad : (h + 1) * ret_pad] = returned[:, h * base : (h + 1) * base]
+
+        def cell_ids(s):
+            return jnp.concatenate(
+                [recv_ref[0, 0, k, s : s + 1, :] for k in range(capacity)], axis=1)
+
         for s in range(air_groups):
-
-            def build(k, _):
-                at = pl.ds(pl.multiple_of(s * span + k * 2 * block, 2 * block), 2 * block)
-                idx = jnp.concatenate(
-                    [recv_ref[0, 0, s, pl.ds(2 * k + i, 1), :] for i in range(2)], axis=1)
-                counts_matrix(cellmat, high, [idx], base, at)
-                looked = mm(ret_bf[...], cellmat[:, at]).astype(BF)
-                for i in range(2):
-                    down_out[s, 2 * k + i] = looked[:, i * block : (i + 1) * block]
-                return _
-
-            lax.fori_loop(0, capacity // 2, build, 0)
+            idx = cell_ids(s)
+            at = slice(s * span, (s + 1) * span)
+            low = as_rows(idx & (base - 1), 16)
+            for t in range(base // 16):
+                lowmat[t * 16 : (t + 1) * 16, at] = low_hot(low, t)
+            found = mm(ret_bf[...], lowmat[:, at])
+            high_of = jnp.broadcast_to(idx >> bits, (ret_pad, span))
+            looked = jnp.zeros((ret_pad, span), F32)
+            for h in range(highs):
+                looked = jnp.where(high_of == h, found[h * ret_pad : (h + 1) * ret_pad], looked)
+            for k in range(capacity):
+                down_out[s, k] = looked[:, k * block : (k + 1) * block].astype(BF)
             down[s].start()
-        take_halo(opool, levels_o, cells)
-        base_p = base_of(omat.shape[0])
-
-        def sweep(c, _):
+        spread[...] = jnp.zeros(spread.shape, BF)
+        base_p = base_of(omat0.shape[0])
+        tiles = cells // width
+
+        def build(c, mat, marks):
             at = pl.ds(pl.multiple_of(c * width, width), width)
-            rows_in = [onbr_ref[0, 0, k : k + 1, at] for k in range(neighbours)]
-            counts_matrix(omat, high, rows_in, base_p, slice(0, width))
-            both = mm(opool[...], omat[...])
-            mean = (both[:levels_o] + both[levels_o:]) * (1.0 / neighbours)
+            rows_in = [onbr_ref[0, k, :, at] for k in range(neighbours)]
+            counts_matrix(mat, marks, rows_in, base_p, slice(0, width))
+
+        def product(c, mat):
+            at = pl.ds(pl.multiple_of(c * width, width), width)
+            mean = mm(opool[...], mat[...]) * (1.0 / neighbours)
             state = sea_ref[0, 0, :, at]
             sea_out[0, 0, :, at] = state + omix_ref[0, :, at] * (mean - state)
+
+        build(0, omat0, high)
+        take_halo(opool, levels_o, cells)
+
+        def pair(i, _):
+            product(2 * i, omat0)
+            build(2 * i + 1, omat1, high1)
+            product(2 * i + 1, omat1)
+            build(2 * i + 2, omat0, high)
             return _
 
-        lax.fori_loop(0, cells // width, sweep, 0)
-        for p in range(partners):
+        lax.fori_loop(0, tiles // 2 - 1, pair, 0)
+        product(tiles - 2, omat0)
+        build(tiles - 1, omat1, high1)
+        product(tiles - 1, omat1)
+        flux = jnp.zeros((highs * field_pad, base), F32)
+        for s in range(air_groups):
             pltpu.make_async_remote_copy(
-                src_ref=up_out.at[p], dst_ref=up_in.at[p], send_sem=x_send.at[p],
-                recv_sem=x_recv.at[p], device_id={"grp": first + p}).wait_recv()
-        tall = min(cells, 512)
-
-        def force(c, _):
-            at = pl.ds(pl.multiple_of(c * tall, tall), tall)
-            flux = jnp.zeros((tall, fields), F32)
-            for s in range(air_groups):
-                flux = flux + lax.dot_general(
-                    cellmat[at, s * span : (s + 1) * span], up_in[s], NT,
-                    preferred_element_type=F32)
+                src_ref=up_out.at[s], dst_ref=up_in.at[s], send_sem=x_send.at[s],
+                recv_sem=x_recv.at[s], device_id={"grp": first + s}).wait_recv()
+            at = slice(s * span, (s + 1) * span)
+            arrived = up_in[s].astype(F32)
+            high_of = jnp.broadcast_to(cell_ids(s) >> bits, (fields, span))
+            for h in range(highs):
+                spread[h * field_pad : h * field_pad + fields, at] = (
+                    jnp.where(high_of == h, arrived, 0.0).astype(BF))
+            flux = flux + lax.dot_general(
+                spread[:, at], lowmat[:, at], NT, preferred_element_type=F32)
+        for h in range(highs):
+            at = slice(h * base, (h + 1) * base)
             sea_out[0, 0, :, at] += lax.dot_general(
-                force_ref[...], flux, NT, precision=EXACT, preferred_element_type=F32)
-            return _
-
-        lax.fori_loop(0, cells // tall, force, 0)
+                force_ref[...], flux[h * field_pad : h * field_pad + fields],
+                (((0,), (0,)), ((), ())), precision=EXACT, preferred_element_type=F32)
         for p in range(partners):
             down[p].wait_send()
 
@@ -306,21 +335,26 @@
     out_specs = (P("grp", "dev", None, None),) * 3
 
     def on_device(*args):
+        args = list(args)
+        args[7] = args[7].transpose(0, 1, 3, 2)
+        args[8] = args[8].transpose(0, 1, 3, 2, 4)
+        args[10] = args[10].transpose(0, 2, 1, 3)
+        args[13] = args[13].T
         air, anbr, asend, _, fw, _, mw, owner, recv, sea, onbr, _, _, _, ret = args
         levels_a, columns = air.shape[2:]
         levels_o, cells = sea.shape[2:]
         half = asend.shape[2] // 2
-        air_groups, capacity, block = recv.shape[2:]
+        capacity, air_groups, block = recv.shape[2:]
         sea_groups = groups - air_groups
         fields, ret_fields = fw.shape[0], ret.shape[0]
         ret_pad = -(-ret_fields // 16) * 16
         row_count = mw.shape[2]
         pool_a, pool_o = columns + 2 * half, cells + 2 * half
         width = 256
+        base, span = base_of(cells), air_groups * capacity * block
         deep = max(
             anbr.shape[2] * (pool_a // base_of(pool_a)),
-            onbr.shape[2] * (pool_o // base_of(pool_o)),
-            cells // base_of(cells),
+            onbr.shape[1] * (pool_o // base_of(pool_o)),
         )
         vmem = pl.BlockSpec(memory_space=pltpu.VMEM)
         smem = pl.BlockSpec(memory_space=pltpu.SMEM)
@@ -330,27 +364,28 @@
         V = pltpu.VMEM
         scratch = [
             V((2, levels, half), BF), V((2, levels, half), BF),
-            V((2 * levels_a, pool_a), BF), V((2 * levels_o, pool_o), BF),
-            V((pool_a, columns), BF), V((pool_o, width), BF),
-            V((columns, row_count), BF), V((cells, air_groups * capacity * block), BF),
-            V((deep, 16, width), BF),
-            V((owner.shape[2], fields, block), F32),
+            V((levels_a, pool_a), BF), V((levels_o, pool_o), BF),
+            V((pool_a, columns), BF), V((pool_o, width), BF), V((pool_o, width), BF),
+            V((columns, row_count), BF), V((base, span), BF),
+            V((cells // base * (-(-fields // 16) * 16), span), BF),
+            V((deep, 16, width), BF), V((deep, 16, width), BF),
+            V((owner.shape[3], fields, block), F32),
             V((sea_groups, fields, capacity * block), BF),
             V((air_groups, fields, capacity * block), BF),
             V((air_groups, capacity, ret_pad, block), BF),
             V((sea_groups, capacity, ret_pad, block), BF),
             V((ret_pad, levels_o), F32),
             V((max(4 * ret_pad, 2 * fields), max(row_count, columns)), BF),
-            V((ret_pad, cells), BF),
+            V((cells // base * ret_pad, base), BF),
             pltpu.SemaphoreType.DMA((2,)), pltpu.SemaphoreType.DMA((2,)),
             pltpu.SemaphoreType.DMA((air_groups,)), pltpu.SemaphoreType.DMA((air_groups,)),
         ]
-        return pl.pallas_call(
+        air_next, sea_next, back = pl.pallas_call(
             functools.partial(kernel, (groups, devs, air_groups)),
             out_shape=(
                 jax.ShapeDtypeStruct(air.shape, F32),
                 jax.ShapeDtypeStruct(sea.shape, F32),
-                jax.ShapeDtypeStruct((1, 1, ret_fields, columns), F32),
+                jax.ShapeDtypeStruct((1, ret_fields, 1, columns), F32),
             ),
             in_specs=ins,
             out_specs=(vmem,) * 3,
@@ -359,6 +394,7 @@
                 collective_id=0, has_side_effects=True, vmem_limit_bytes=60 * 1024 * 1024),
             name="couple",
         )(*args)
+        return air_next, sea_next, back.transpose(0, 2, 1, 3)
 
     return jax.shard_map(
         on_device, mesh=mesh, in_specs=in_specs, out_specs=out_specs, check_vma=False)

time: 36.2 us -> 24.6 us (0.68)
  Pallas kernels: 26.1 us -> 20.3 us
  local copies, waits for them, and re-layouts: 9.01 us -> 3.41 us
    pallas_call x1, Pallas kernels: 26.1 us -> 20.3 us  [on_device(): pl.pallas_call(functools.partial(kernel, (groups, devs, air_groups)), out...]
    unnamed x10 -> x7, local copies, waits for them, and re-layouts: 7.44 us -> 3.41 us
    pallas_call x1 -> x0, local copies, waits for them, and re-layouts: 1.57 us -> none  [on_device(): pl.pallas_call(functools.partial(kernel, (groups, devs, air_groups)), out...]
where the time goes in v2:
time: 24.6 us; the launch traced here: 24.4 us
  Pallas kernels  20.3 us (83%)
  local copies, waits for them, and re-layouts  3.41 us (14%)
  between operations  0.66 us (3%)
    pallas_call x1, Pallas kernels, on_device(): pl.pallas_call(functools.partial(kernel, (groups, devs, air_groups)), out...  20.3 us
    unnamed x7, local copies, waits for them, and re-layouts  3.41 us

profile of v2, /device:TPU:28, one launch (start us, length us, event | category | flops | bytes accessed | tf_op | source)
XLA Modules:
  0.0 24.4 jit_solution(10126919799348959415)
XLA Ops:
  0.6 20.3 %couple.1 = (f32[1,1,128,1024]{3,2,1,0:T(8,128)}, f32[1,1,80,2048]{3,2,1,0:T(8,128)}, f32[1,12,1,1024]{3,2,1,0:T(1,128)}) custom-call(f32[1,1,128,1024]{3,2,1,0:T(8,128)} %air_ref.1, s32[1,1,4,1024]{3,2,1,0:T(4,128)} %anbr_ref.1, s32[1,1,256]{2,1,0:T(1,128)} %asend_ref.1, f32[1,1,1024]{2,1,0:T(1,128)} %amix_ref.1, f32[24,128]{1,0:T(8,128)} %fw_ref.1, ...), custom_call_target="tpu_custom_call" | custom-call | tf_op jit(solution)/shard_map/couple/pallas_call | solution.py:383
  21.0 0.0 copy-start
  21.0 1.9 %copy.22 = f32[1,1,128,1024]{3,2,1,0:T(8,128)} copy(f32[1,1,128,1024]{3,2,1,0:T(8,128)} %get-tuple-element.15) | data formatting | bytes 1048576
  23.0 0.0 copy-done
  23.0 0.0 copy-start.1
  23.0 0.8 %copy.23 = f32[1,1,80,2048]{3,2,1,0:T(8,128)} copy(f32[1,1,80,2048]{3,2,1,0:T(8,128)S(1)} %copy-done) | data formatting | bytes 1310720
  23.8 0.0 copy-done.1
  23.8 0.6 %copy.24 = f32[1,1,12,1024]{3,1,2,0:T(1,128)} copy(f32[1,1,12,1024]{3,1,2,0:T(1,128)S(1)} %bitcast.8) | data formatting | bytes 98304
Async XLA Ops:
  21.0 2.0 %copy-start = (f32[1,1,80,2048]{3,2,1,0:T(8,128)S(1)}, f32[1,1,80,2048]{3,2,1,0:T(8,128)}, u32[]{:S(2)}) copy-start(f32[1,1,80,2048]{3,2,1,0:T(8,128)} %get-tuple-element.16) | copy-start | bytes 1966084
  23.0 0.8 %copy-start.1 = (f32[1,12,1,1024]{3,2,1,0:T(1,128)S(1)}, f32[1,12,1,1024]{3,2,1,0:T(1,128)}, u32[]{:S(2)}) copy-start(f32[1,12,1,1024]{3,2,1,0:T(1,128)} %get-tuple-element.8) | copy-start | bytes 147460
